TPU v7x, 32 devices: a whole 2x2x4 slice. The times are simulated.
32 devices in a mesh: groups: 2 (over y), seq: 4 (over z), fsdp: 2 (over x), sub: 2 (over core).
Axes of the slice: x: 2, y: 2, z: 4, core: 2. Of those that a mesh axis runs over, the one named last changes fastest.
Arguments:
- tokens: bfloat16 [2048, 8192], P(('groups', 'seq')), parts along dimension 0, may hold values from -400 to 400
- norm_gain: float32 [8192], replicated, may hold values from 0.1 to 1.9
- w_query: bfloat16 [8, 16, 8192], P(('seq', 'sub'), 'fsdp'), may hold values from -0.0625 to 0.0625
- w_key: bfloat16 [8, 16, 8192], P(('seq', 'sub'), 'fsdp'), may hold values from -0.0625 to 0.0625
- w_value: bfloat16 [8, 128, 8192], P(('seq', 'sub'), 'fsdp'), may hold values from -5 to 5
- head_gain: float32 [128], replicated, may hold values from 0.1 to 1.9
- w_out: bfloat16 [8, 128, 8192], P('seq', None, ('fsdp', 'sub')), may hold values from -0.1875 to 0.1875
Outputs:
- mixed: bfloat16 [2048, 8192], P(('groups', 'seq'), ('fsdp', 'sub')), parts along dimension 0
There are 2 independent parts, one for each index of `groups`. A program takes and returns all parts, laid end to end along the dimension named above; an argument that names none is the same for every part. Nothing has to cross between parts.
All inputs are finite; a program needn't handle non-finite values.
Results may differ from a plain program's by a relative error of at most 0.0084.
Values may be sent and summed in bfloat16 or wider, within the bound.
No kernel may reach another device: no remote copies, remote signals or barrier semaphores. Data moves between devices by JAX's collectives and lax.ppermute only.
A program may use at most 64 MiB of HBM per device.

v0:
```python
import math
import jax
import jax.numpy as jnp
import numpy as np
from jax import lax
from jax.sharding import PartitionSpec as P

BLOCK = 512


def taylor_first(vectors):
    feature_count = vectors.shape[0]
    first_row, second_row = np.triu_indices(feature_count, 1)
    cross_terms = vectors[first_row] * vectors[second_row] / 4.0
    squares = vectors * vectors / (4.0 * math.sqrt(2.0))
    leading = jnp.ones((1,) + vectors.shape[1:], jnp.float32)
    return jnp.concatenate([leading, vectors / 2.0, cross_terms, squares], 0)


def head_norm(numerator, head_gain, channel_axis):
    widened = numerator.astype(jnp.float32)
    meansq = jnp.mean(widened * widened, axis=channel_axis, keepdims=True)
    gain_shape = tuple((-1 if axis_pos == channel_axis else 1 for axis_pos in range(widened.ndim)))
    return (widened * lax.rsqrt(meansq + 1e-06) * head_gain.reshape(gain_shape)).astype(
        jnp.bfloat16
    )


def attend(queries, key_vectors, values_local):
    length = queries.shape[1]
    nblocks = length // BLOCK
    channels = values_local.shape[0]
    query_feats = taylor_first(queries.astype(jnp.float32)).astype(jnp.bfloat16)
    key_feats = taylor_first(key_vectors.astype(jnp.float32)).astype(jnp.bfloat16)
    taylor_width = query_feats.shape[0]
    contrib = jnp.einsum(
        "fbj,ebj->bfe",
        key_feats.reshape(taylor_width, nblocks, BLOCK),
        values_local.reshape(channels, nblocks, BLOCK),
        preferred_element_type=jnp.float32,
    )
    prefix = jnp.concatenate([jnp.zeros_like(contrib[:1]), jnp.cumsum(contrib[:-1], axis=0)], 0)
    prior_state = prefix.astype(jnp.bfloat16)
    carried = jnp.einsum(
        "bfe,fbt->bet",
        prior_state,
        query_feats.reshape(taylor_width, nblocks, BLOCK),
        preferred_element_type=jnp.float32,
    )
    earlier = lax.broadcasted_iota(jnp.int32, (BLOCK, BLOCK), 0)
    column_pos = lax.broadcasted_iota(jnp.int32, (BLOCK, BLOCK), 1)
    causal = earlier <= column_pos

    def one_block(block_index):
        offset = block_index * BLOCK
        query_block = lax.dynamic_slice_in_dim(queries, offset, BLOCK, 1)
        key_block = lax.dynamic_slice_in_dim(key_vectors, offset, BLOCK, 1)
        value_block = lax.dynamic_slice_in_dim(values_local, offset, BLOCK, 1)
        scores = jnp.einsum("fj,ft->jt", key_block, query_block, preferred_element_type=jnp.float32)
        kernel = 1.0 + scores / 4.0 + scores * scores / 32.0
        weight = jnp.where(causal, kernel, 0.0).astype(jnp.bfloat16)
        return jnp.einsum("ej,jt->et", value_block, weight, preferred_element_type=jnp.float32)

    local_part = lax.map(one_block, jnp.arange(nblocks, dtype=jnp.int32))
    numerator = (local_part + carried).astype(jnp.bfloat16)
    return jnp.transpose(numerator, (1, 0, 2)).reshape(channels, length)


def per_device(tokens, norm_gain, w_query, w_key, w_value, head_gain, w_out):
    feat_dev = w_query.shape[1]
    inputs = tokens.astype(jnp.float32)
    meansq = jnp.mean(inputs * inputs, axis=1, keepdims=True)
    normed = (inputs * lax.rsqrt(meansq + 1e-05) * norm_gain).astype(jnp.bfloat16)
    stacked = jnp.concatenate([w_query, w_key, w_value], 1)
    head_weights, out_weights = (
        lax.all_gather(stacked, "seq", axis=0, tiled=True),
        lax.all_gather(w_out, "seq", axis=0, tiled=True),
    )
    projected = jnp.einsum(
        "hcd,td->hct", head_weights, normed, preferred_element_type=jnp.float32
    ).astype(jnp.bfloat16)
    by_head = lax.all_to_all(projected, "seq", split_axis=0, concat_axis=2, tiled=True)
    qk_local = by_head[:, : 2 * feat_dev]
    values_local = by_head[0, 2 * feat_dev :]
    qk_whole = lax.all_gather(qk_local, "fsdp", axis=0, tiled=True)
    length = qk_whole.shape[2]
    queries = qk_whole[:, :feat_dev].reshape(-1, length)
    key_vectors = qk_whole[:, feat_dev:].reshape(-1, length)
    numerator = attend(queries, key_vectors, values_local)
    heads_total = out_weights.shape[0]
    head_width = out_weights.shape[1]
    by_token = lax.all_to_all(numerator[None], "seq", split_axis=2, concat_axis=0, tiled=True)
    everyone = lax.all_gather(by_token[None], ("fsdp", "sub"), axis=0, tiled=True)
    arranged = everyone.reshape(
        lax.axis_size("fsdp"),
        lax.axis_size("sub"),
        everyone.shape[1],
        everyone.shape[2],
        everyone.shape[3],
    )
    arranged = jnp.transpose(arranged, (2, 1, 0, 3, 4)).reshape(heads_total, head_width, -1)
    attended = head_norm(arranged, head_gain, 1)
    mixed = jnp.einsum("het,hed->td", attended, out_weights, preferred_element_type=jnp.float32)
    return mixed.astype(jnp.bfloat16)


def solution(mesh):
    in_specs = (
        P(("groups", "seq"), None),
        P(),
        P(("seq", "sub"), "fsdp", None),
        P(("seq", "sub"), "fsdp", None),
        P(("seq", "sub"), "fsdp", None),
        P(),
        P("seq", None, ("fsdp", "sub")),
    )
    out_specs = P(("groups", "seq"), ("fsdp", "sub"))
    return jax.shard_map(
        per_device, mesh=mesh, in_specs=in_specs, out_specs=out_specs, check_vma=False
    )
```

profile of v0, /device:TPU:0, one launch (start us, length us, event | category | flops | bytes accessed | tf_op | source)
XLA Modules:
  0.0 208.2 jit_solution(16304550115294808762)
XLA Ops:
  6.5 2.5 %pad_maximum_fusion = bf16[1,80,8192]{2,1,0:T(8,128)(2,1)} fusion(bf16[1,64,8192]{2,1,0:T(8,128)(2,1)} %param.21, bf16[1,8,8192]{2,1,0:T(8,128)(2,1)} %param.20, bf16[1,8,8192]{2,1,0:T(8,128)(2,1)} %param.19), kind=kLoop, calls=%fused_computation.32 | loop fusion | flops 3932160 | bytes 2621440 | tf_op jit(solution)/shard_map/concatenate | solution.py:74
  9.1 0.7 all-gather.6.cloned.1.call-update
  9.8 3.1 %fusion.18 = f32[256]{0:T(256)S(1)} fusion(bf16[256,8192]{1,0:T(8,128)(2,1)} %param.17), kind=kLoop, calls=%fused_computation.23 | loop fusion | flops 6291200 | bytes 4195328 | tf_op jit(solution)/shard_map/reduce_sum | solution.py:72
  12.9 97.0 %all-gather.4.cloned.1.call-done = bf16[4,80,8192]{2,1,0:T(8,128)(2,1)} async-done(((bf16[1,80,8192]{2,1,0:T(8,128)(2,1)}), bf16[4,80,8192]{2,1,0:T(8,128)(2,1)}) %all-gather.4.cloned.1.call-update) | async-done | bytes 5242896 | tf_op jit(solution)/shard_map/all_gather | solution.py:76
  110.0 6.1 %fusion.27 = bf16[4,80,256]{2,1,0:T(8,128)(2,1)} fusion(bf16[4,80,8192]{2,1,0:T(8,128)(2,1)} %all-gather.4.cloned.1.call-done, bf16[256,8192]{1,0:T(8,128)(2,1)} %param.17, f32[8192]{0:T(1024)S(1)} %copy-done.2, f32[256]{0:T(256)S(1)} %add_rsqrt_fusion), kind=kOutput, calls=%fused_computation.34 | convolution fusion | flops 1350647808 | bytes 9634816 | tf_op jit(solution)/shard_map/hcd,td->hct/dot_general | solution.py:79
  116.0 3.3 %all-to-all-start = ((bf16[4,80,256]{2,1,0:T(8,128)(2,1)}), bf16[4,80,256]{2,1,0:T(8,128)(2,1)S(1)}, u32[]{:S(2)}, u32[]{:S(2)}) async-start(bf16[4,80,256]{2,1,0:T(8,128)(2,1)} %fusion.27), calls=%async_computation | async-start | bytes 327680 | tf_op jit(solution)/shard_map/all_to_all | solution.py:82
  119.5 11.4 %all-to-all-done = bf16[4,80,256]{2,1,0:T(8,128)(2,1)S(1)} async-done(((bf16[4,80,256]{2,1,0:T(8,128)(2,1)}), bf16[4,80,256]{2,1,0:T(8,128)(2,1)S(1)}, u32[]{:S(2)}, u32[]{:S(2)}) %all-to-all-start) | async-done | bytes 163872 | tf_op jit(solution)/shard_map/all_to_all | solution.py:82
  130.9 4.6 %all_gather.13 = bf16[2,16,1024]{2,1,0:T(8,128)(2,1)S(1)} all-gather(bf16[1,16,1024]{2,1,0:T(8,128)(2,1)S(1)} %slice.30), channel_id=1, replica_groups=mesh['groups'=2,'seq'=4,'fsdp'=2,'sub'=2] {'fsdp'}, dimensions={0}, use_global_device_ids=true | all-gather | bytes 98304 | tf_op jit(solution)/shard_map/all_gather | solution.py:85
  135.5 0.8 gather_fusion
  136.3 0.8 gather_fusion.1
  137.1 0.8 gather_fusion.2
  137.9 0.8 gather_fusion.3
  139.5 3.5 %while.11 = (s32[]{:T(128)}, f32[2,64,512]{2,1,0:T(8,128)S(1)}, s32[2]{0:T(128)S(1)}, bf16[64,1024]{1,0:T(8,128)(2,1)S(1)}, bf16[16,1024]{1,0:T(8,128)(2,1)S(1)}...) while((s32[]{:T(128)}, f32[2,64,512]{2,1,0:T(8,128)S(1)}, ...), condition=%wide.region_2.3_spmd.clone, body=%wide.region_1.0_spmd.clone.sunk | while | flops 44040196 | bytes 231075 | solution.py:64
  139.5 0.6 dynamic_slice.32
  140.7 0.5 fusion.70
  141.2 0.6 dynamic_slice.32
  142.5 0.5 fusion.70
  143.6 0.5 broadcast.135
  144.1 2.3 %reduce.7 = bf16[1024,64]{1,0:T(8,128)(2,1)S(1)} reduce(bf16[1024,1,64]{2,1,0:T(2,128)(2,1)S(1)} %bitcast.63, bf16[]{:T(256)} %broadcast.135), dimensions={1}, to_apply=%bitcast.51.reduce_sub_computation | reduce | bytes 262146
  146.6 13.8 %all_to_all.33 = bf16[4,2,8192]{2,1,0:T(2,128)(2,1)S(1)} all-to-all(bf16[4,2,8192]{2,1,0:T(2,128)(2,1)S(1)} %reshape.137), channel_id=1, replica_groups=mesh['groups'=2,'seq'=4,'fsdp'=2,'sub'=2] {'seq'}, dimensions={0} | all-to-all | bytes 262144 | tf_op jit(solution)/shard_map/all_to_all | solution.py:92
  160.8 0.3 copy.76
  161.2 7.1 %all-gather = bf16[16,1,64,256]{3,2,1,0:T(8,128)(2,1)S(1)} all-gather(bf16[4,1,64,256]{3,2,1,0:T(8,128)(2,1)S(1)} %copy.77), channel_id=2, replica_groups=mesh['groups'=2,'seq'=4,'fsdp'=2,'sub'=2] {'fsdp','sub'}, dimensions={0}, use_global_device_ids=true | all-gather | bytes 655360 | tf_op jit(solution)/shard_map/all_gather | solution.py:93
  168.8 28.0 %all-gather.6.cloned.1.call-done = bf16[8,128,2048]{2,1,0:T(8,128)(2,1)} async-done(((bf16[2,128,2048]{2,1,0:T(8,128)(2,1)}), bf16[8,128,2048]{2,1,0:T(8,128)(2,1)}) %all-gather.6.cloned.1.call-update) | async-done | bytes 4194320 | tf_op jit(solution)/shard_map/all_gather | solution.py:77
  196.8 4.5 %fusion.26 = bf16[256,2048]{1,0:T(8,128)(2,1)} fusion(bf16[8,128,2048]{2,1,0:T(8,128)(2,1)} %all-gather.6.cloned.1.call-done, f32[8,128,256]{2,1,0:T(8,128)S(1)} %bitcast.64, f32[128]{0:T(128)S(1)} %copy-done.3, f32[8,256]{1,0:T(8,128)S(1)} %rsqrt.21), kind=kOutput, calls=%fused_computation.31 | convolution fusion | flops 1075052544 | bytes 6300160 | tf_op jit(solution)/shard_map/het,hed->td/dot_general | solution.py:103
  (51 shorter events, 2.4 us)
Async XLA Ops:
  6.5 103.4 %copy-start.2 = (f32[8192]{0:T(1024)S(1)}, f32[8192]{0:T(1024)}, u32[]{:S(2)}) copy-start(f32[8192]{0:T(1024)} %param.18) | copy-start | bytes 98308
  6.5 103.4 %all-gather.4.cloned.1.call-start = ((), (), s32[]{:S(2)}) async-start(), calls=%async_computation.2 | async-start | bytes 6553600 | tf_op jit(solution)/shard_map/all_gather | solution.py:76
  9.0 187.8 %all-gather.6.cloned.1.call-start = ((), (), s32[]{:S(2)}) async-start(), calls=%async_computation.3 | async-start | bytes 5242880 | tf_op jit(solution)/shard_map/all_gather | solution.py:77
  12.9 106.5 %copy-start.1 = (s32[120]{0:T(128)S(1)}, s32[120]{0:T(128)}, u32[]{:S(2)}) copy-start(s32[120]{0:T(128)} %constant.78) | copy-start | bytes 1444
  12.9 106.5 %copy-start = (s32[120]{0:T(128)S(1)}, s32[120]{0:T(128)}, u32[]{:S(2)}) copy-start(s32[120]{0:T(128)} %constant.79) | copy-start | bytes 1444
  116.0 14.8 %all-to-all-start = ((bf16[4,80,256]{2,1,0:T(8,128)(2,1)}), bf16[4,80,256]{2,1,0:T(8,128)(2,1)S(1)}, u32[]{:S(2)}, u32[]{:S(2)}) async-start(bf16[4,80,256]{2,1,0:T(8,128)(2,1)} %fusion.27), calls=%async_computation | async-start | bytes 327680 | tf_op jit(solution)/shard_map/all_to_all | solution.py:82
  143.6 53.3 %copy-start.3 = (f32[128]{0:T(128)S(1)}, f32[128]{0:T(128)}, u32[]{:S(2)}) copy-start(f32[128]{0:T(128)} %param.22) | copy-start | bytes 1540
Sparse Core Ops, SparseCore 0:
  9.2 100.7 all-gather.3
  111.5 85.2 all-gather.5
where the time goes:
time: 209 us; the launch traced here: 208 us
  waiting for transfers between devices  137 us (66%)
  blocking collectives  25.6 us (12%)
  between operations  13.8 us (7%)
  matrix products  12.1 us (6%)
  other arithmetic  8.29 us (4%)
  local copies, waits for them, and re-layouts  6.51 us (3%)
  starting transfers between devices  3.39 us (2%)
    all_gather x1, waiting for transfers between devices, per_device(): lax.all_gather(stacked, 'seq', axis=0, tiled=True)  97 us
    all_gather x1, waiting for transfers between devices, per_device(): lax.all_gather(w_out, 'seq', axis=0, tiled=True)  28 us
    all_to_all x1, blocking collectives, per_device(): lax.all_to_all(numerator[None], 'seq', split_axis=2, concat_axis=0, tiled...  13.8 us
    all_to_all x1, waiting for transfers between devices, per_device(): lax.all_to_all(projected, 'seq', split_axis=0, concat_axis=2, tiled=True)  11.4 us
    all_gather x1, blocking collectives, per_device(): lax.all_gather(by_token[None], ('fsdp', 'sub'), axis=0, tiled=True)  7.15 us
    dot_general x1, matrix products, per_device(): jnp.einsum('hcd,td->hct', head_weights, normed, preferred_element_type=jn...  6.07 us
    all_gather x1, blocking collectives, per_device(): qk_whole = lax.all_gather(qk_local, 'fsdp', axis=0, tiled=True)  4.58 us
    dot_general x1, matrix products, per_device(): jnp.einsum('het,hed->td', attended, out_weights, preferred_element_type=j...  4.52 us
  transfers between devices with their start and end apart: 3, of which 3 were waited for; matrix products, arithmetic and copies ran while one was open for 10% of the time, Pallas kernels for 0%

commit v1 on v0

--- a/solution.py
+++ b/solution.py
@@ -89,7 +89,12 @@
     numerator = attend(queries, key_vectors, values_local)
     heads_total = out_weights.shape[0]
     head_width = out_weights.shape[1]
-    by_token = lax.all_to_all(numerator[None], "seq", split_axis=2, concat_axis=0, tiled=True)
+    by_token = jnp.concatenate(
+        lax.all_to_all(
+            jnp.stack(jnp.split(numerator[None], lax.axis_size("seq"), axis=2)), "seq", 0, 0
+        ),
+        axis=0,
+    )
     everyone = lax.all_gather(by_token[None], ("fsdp", "sub"), axis=0, tiled=True)
     arranged = everyone.reshape(
         lax.axis_size("fsdp"),

time: 209 us -> 209 us (level)
  waiting for transfers between devices: 137 us -> 140 us
  other arithmetic: 8.29 us -> 6.04 us
    all_gather x1, waiting for transfers between devices: 28 us -> 30.6 us  [per_device(): lax.all_gather(w_out, 'seq', axis=0, tiled=True)]
    unnamed x1 -> x0, other arithmetic: 2.27 us -> none
  transfers between devices with their start and end apart: 3 -> 3, of which waited for: 3 -> 3; matrix products, arithmetic and copies ran while one was open for 10% -> 8% of each run, Pallas kernels for 0% -> 0%
where the time goes in v1:
time: 209 us; the launch traced here: 208 us
  waiting for transfers between devices  140 us (67%)
  blocking collectives  26.9 us (13%)
  between operations  13.7 us (7%)
  matrix products  12.1 us (6%)
  other arithmetic  6.04 us (3%)
  local copies, waits for them, and re-layouts  4.94 us (2%)
  starting transfers between devices  3.39 us (2%)
    all_gather x1, waiting for transfers between devices, per_device(): lax.all_gather(stacked, 'seq', axis=0, tiled=True)  97 us
    all_gather x1, waiting for transfers between devices, per_device(): lax.all_gather(w_out, 'seq', axis=0, tiled=True)  30.6 us
    all_to_all x1, blocking collectives, per_device(): lax.all_to_all(jnp.stack(jnp.split(numerator[None], lax.axis_size('seq'),...  15.1 us
    all_to_all x1, waiting for transfers between devices, per_device(): lax.all_to_all(projected, 'seq', split_axis=0, concat_axis=2, tiled=True)  11.4 us
    all_gather x1, blocking collectives, per_device(): lax.all_gather(by_token[None], ('fsdp', 'sub'), axis=0, tiled=True)  7.19 us
    dot_general x1, matrix products, per_device(): jnp.einsum('hcd,td->hct', head_weights, normed, preferred_element_type=jn...  6.07 us
    all_gather x1, blocking collectives, per_device(): qk_whole = lax.all_gather(qk_local, 'fsdp', axis=0, tiled=True)  4.58 us
    dot_general x1, matrix products, per_device(): jnp.einsum('het,hed->td', attended, out_weights, preferred_element_type=j...  4.52 us
  transfers between devices with their start and end apart: 3, of which 3 were waited for; matrix products, arithmetic and copies ran while one was open for 8% of the time, Pallas kernels for 0%

profile of v1, /device:TPU:0, one launch (start us, length us, event | category | flops | bytes accessed | tf_op | source)
XLA Modules:
  0.0 208.2 jit_solution(15778652284450286756)
XLA Ops:
  6.5 2.5 %pad_maximum_fusion = bf16[1,80,8192]{2,1,0:T(8,128)(2,1)} fusion(bf16[1,64,8192]{2,1,0:T(8,128)(2,1)} %param.21, bf16[1,8,8192]{2,1,0:T(8,128)(2,1)} %param.20, bf16[1,8,8192]{2,1,0:T(8,128)(2,1)} %param.19), kind=kLoop, calls=%fused_computation.32 | loop fusion | flops 3932160 | bytes 2621440 | tf_op jit(solution)/shard_map/concatenate | solution.py:74
  9.1 0.7 all-gather.6.cloned.1.call-update
  9.8 3.1 %fusion.18 = f32[256]{0:T(256)S(1)} fusion(bf16[256,8192]{1,0:T(8,128)(2,1)} %param.17), kind=kLoop, calls=%fused_computation.23 | loop fusion | flops 6291200 | bytes 4195328 | tf_op jit(solution)/shard_map/reduce_sum | solution.py:72
  12.9 97.0 %all-gather.4.cloned.1.call-done = bf16[4,80,8192]{2,1,0:T(8,128)(2,1)} async-done(((bf16[1,80,8192]{2,1,0:T(8,128)(2,1)}), bf16[4,80,8192]{2,1,0:T(8,128)(2,1)}) %all-gather.4.cloned.1.call-update) | async-done | bytes 5242896 | tf_op jit(solution)/shard_map/all_gather | solution.py:76
  110.0 6.1 %fusion.27 = bf16[4,80,256]{2,1,0:T(8,128)(2,1)} fusion(bf16[4,80,8192]{2,1,0:T(8,128)(2,1)} %all-gather.4.cloned.1.call-done, bf16[256,8192]{1,0:T(8,128)(2,1)} %param.17, f32[8192]{0:T(1024)S(1)} %copy-done.2, f32[256]{0:T(256)S(1)} %add_rsqrt_fusion), kind=kOutput, calls=%fused_computation.34 | convolution fusion | flops 1350647808 | bytes 9634816 | tf_op jit(solution)/shard_map/hcd,td->hct/dot_general | solution.py:79
  116.0 3.3 %all-to-all-start = ((bf16[4,80,256]{2,1,0:T(8,128)(2,1)}), bf16[4,80,256]{2,1,0:T(8,128)(2,1)S(1)}, u32[]{:S(2)}, u32[]{:S(2)}) async-start(bf16[4,80,256]{2,1,0:T(8,128)(2,1)} %fusion.27), calls=%async_computation | async-start | bytes 327680 | tf_op jit(solution)/shard_map/all_to_all | solution.py:82
  119.5 11.4 %all-to-all-done = bf16[4,80,256]{2,1,0:T(8,128)(2,1)S(1)} async-done(((bf16[4,80,256]{2,1,0:T(8,128)(2,1)}), bf16[4,80,256]{2,1,0:T(8,128)(2,1)S(1)}, u32[]{:S(2)}, u32[]{:S(2)}) %all-to-all-start) | async-done | bytes 163872 | tf_op jit(solution)/shard_map/all_to_all | solution.py:82
  130.9 4.6 %all_gather.13 = bf16[2,16,1024]{2,1,0:T(8,128)(2,1)S(1)} all-gather(bf16[1,16,1024]{2,1,0:T(8,128)(2,1)S(1)} %slice.30), channel_id=1, replica_groups=mesh['groups'=2,'seq'=4,'fsdp'=2,'sub'=2] {'fsdp'}, dimensions={0}, use_global_device_ids=true | all-gather | bytes 98304 | tf_op jit(solution)/shard_map/all_gather | solution.py:85
  135.5 0.8 gather_fusion
  136.3 0.8 gather_fusion.1
  137.1 0.8 gather_fusion.2
  137.9 0.8 gather_fusion.3
  139.2 0.3 fusion.34
  139.5 3.5 %while.11 = (s32[]{:T(128)}, f32[2,64,512]{2,1,0:T(8,128)S(1)}, s32[2]{0:T(128)S(1)}, bf16[64,1024]{1,0:T(8,128)(2,1)S(1)}, bf16[16,1024]{1,0:T(8,128)(2,1)S(1)}...) while((s32[]{:T(128)}, f32[2,64,512]{2,1,0:T(8,128)S(1)}, ...), condition=%wide.region_2.3_spmd.clone, body=%wide.region_1.0_spmd.clone.sunk | while | flops 44040196 | bytes 231075 | solution.py:64
  139.5 0.6 dynamic_slice.32
  140.7 0.5 fusion.70
  141.2 0.6 dynamic_slice.32
  142.5 0.5 fusion.70
  143.0 0.3 fusion.31
  143.2 0.1 copy.65
  143.5 15.1 %all_to_all.23 = bf16[4,1,64,256]{3,2,1,0:T(8,128)(2,1)S(1)} all-to-all(bf16[4,1,64,256]{3,2,1,0:T(8,128)(2,1)S(1)} %pad_maximum_fusion.1), channel_id=1, replica_groups=mesh['groups'=2,'seq'=4,'fsdp'=2,'sub'=2] {'seq'}, dimensions={0} | all-to-all | bytes 262144 | tf_op jit(solution)/shard_map/all_to_all | solution.py:93
  158.6 7.2 %all-gather = bf16[16,1,64,256]{3,2,1,0:T(8,128)(2,1)S(1)} all-gather(bf16[4,1,64,256]{3,2,1,0:T(8,128)(2,1)S(1)} %all_to_all.23), channel_id=2, replica_groups=mesh['groups'=2,'seq'=4,'fsdp'=2,'sub'=2] {'fsdp','sub'}, dimensions={0}, use_global_device_ids=true | all-gather | bytes 655360 | tf_op jit(solution)/shard_map/all_gather | solution.py:98
  166.3 30.6 %all-gather.6.cloned.1.call-done = bf16[8,128,2048]{2,1,0:T(8,128)(2,1)} async-done(((bf16[2,128,2048]{2,1,0:T(8,128)(2,1)}), bf16[8,128,2048]{2,1,0:T(8,128)(2,1)}) %all-gather.6.cloned.1.call-update) | async-done | bytes 4194320 | tf_op jit(solution)/shard_map/all_gather | solution.py:77
  196.8 4.5 %fusion.26 = bf16[256,2048]{1,0:T(8,128)(2,1)} fusion(bf16[8,128,2048]{2,1,0:T(8,128)(2,1)} %all-gather.6.cloned.1.call-done, f32[8,128,256]{2,1,0:T(8,128)S(1)} %bitcast.65, f32[128]{0:T(128)S(1)} %copy-done.3, f32[8,256]{1,0:T(8,128)S(1)} %rsqrt.21), kind=kOutput, calls=%fused_computation.31 | convolution fusion | flops 1075052544 | bytes 6300160 | tf_op jit(solution)/shard_map/het,hed->td/dot_general | solution.py:108
  (46 shorter events, 1.0 us)
Async XLA Ops:
  6.5 103.4 %copy-start.2 = (f32[8192]{0:T(1024)S(1)}, f32[8192]{0:T(1024)}, u32[]{:S(2)}) copy-start(f32[8192]{0:T(1024)} %param.18) | copy-start | bytes 98308
  6.5 103.4 %all-gather.4.cloned.1.call-start = ((), (), s32[]{:S(2)}) async-start(), calls=%async_computation.2 | async-start | bytes 6553600 | tf_op jit(solution)/shard_map/all_gather | solution.py:76
  9.0 187.8 %all-gather.6.cloned.1.call-start = ((), (), s32[]{:S(2)}) async-start(), calls=%async_computation.3 | async-start | bytes 5242880 | tf_op jit(solution)/shard_map/all_gather | solution.py:77
  12.9 106.5 %copy-start.1 = (s32[120]{0:T(128)S(1)}, s32[120]{0:T(128)}, u32[]{:S(2)}) copy-start(s32[120]{0:T(128)} %constant.78) | copy-start | bytes 1444
  12.9 106.5 %copy-start = (s32[120]{0:T(128)S(1)}, s32[120]{0:T(128)}, u32[]{:S(2)}) copy-start(s32[120]{0:T(128)} %constant.79) | copy-start | bytes 1444
  116.0 14.8 %all-to-all-start = ((bf16[4,80,256]{2,1,0:T(8,128)(2,1)}), bf16[4,80,256]{2,1,0:T(8,128)(2,1)S(1)}, u32[]{:S(2)}, u32[]{:S(2)}) async-start(bf16[4,80,256]{2,1,0:T(8,128)(2,1)} %fusion.27), calls=%async_computation | async-start | bytes 327680 | tf_op jit(solution)/shard_map/all_to_all | solution.py:82
  142.9 53.9 %copy-start.3 = (f32[128]{0:T(128)S(1)}, f32[128]{0:T(128)}, u32[]{:S(2)}) copy-start(f32[128]{0:T(128)} %param.22) | copy-start | bytes 1540
Sparse Core Ops, SparseCore 0:
  9.2 100.7 all-gather.3
  111.5 85.2 all-gather.5
